TPU v7x, 32 devices: a whole 2x2x4 slice. The times are simulated.
32 devices in a mesh: dp: 4 (over y, x), row: 2 (over core), col: 4 (over z).
Axes of the slice: x: 2, y: 2, z: 4, core: 2. Of those that a mesh axis runs over, the one named last changes fastest.
Arguments:
- hidden_state_input: bfloat16 [2048, 1024], P('dp', 'col'), may hold values from -6 to 6
- initial_token_embedding: bfloat16 [2048, 1024], P('dp', 'col'), may hold values from -6 to 6
- document_numbers: int32 [2048], P('dp'), may hold values from 0 to 3, as said below
- document_start_flags: int32 [2048], P('dp'), may hold values from 0 to 1, as said below
- attention_norm_gain: float32 [2, 1024], P(None, 'col'), may hold values from 0.5 to 1.5
- query_key_value_matrix: bfloat16 [3, 2, 1024, 2048], P(None, None, 'col', 'row'), may hold values from -0.125 to 0.125
- attention_out_matrix: bfloat16 [2048, 2, 1024], P('row', None, 'col'), may hold values from -1 to 1
- perceptron_norm_gain: float32 [2, 1024], P(None, 'col'), may hold values from 0.5 to 1.5
- gate_up_matrix: bfloat16 [2, 2, 1024, 4096], P(None, None, 'col', 'row'), may hold values from -0.125 to 0.125
- adapter_down: bfloat16 [2, 1024, 128], P(None, 'col'), may hold values from -0.125 to 0.125
- adapter_up: bfloat16 [2, 128, 4096], P(None, None, ('row', 'col')), may hold values from -0.25 to 0.25
- down_matrix: bfloat16 [4096, 2, 1024], P('row', None, 'col'), may hold values from -0.09375 to 0.09375
- projection_matrix: bfloat16 [2, 1024, 1024], P(None, 'col'), may hold values from -0.125 to 0.125
- mixer_norm_gain: float32 [1024], P('col'), may hold values from 0.5 to 1.5
- gate_in_matrix: bfloat16 [2, 1024, 2048], P(None, 'col', 'row'), may hold values from -0.1875 to 0.1875
- state_in_matrix: bfloat16 [1024, 160], P('col'), may hold values from -0.1875 to 0.1875
- mixer_input_kernel: float32 [4, 2048], P(None, ('row', 'col')), may hold values from -3 to 3
- state_conv_kernel: float32 [4, 128], replicated, may hold values from -3 to 3
- step_offset_bias: float32 [32], P(('row', 'col')), may hold values from -4 to -1
- log_decay_rates: float32 [32], P(('row', 'col')), may hold values from 0 to 2.5
- head_skip_term: float32 [32], P(('row', 'col')), may hold values from 0.5 to 1.5
- gated_norm_gain: float32 [2048], P(('row', 'col')), may hold values from 0.5 to 1.5
- mixer_out_matrix: bfloat16 [2048, 1024], P('row', 'col'), may hold values from -0.125 to 0.125
- output_gradient: bfloat16 [2048, 1024], P('dp', 'col'), may hold values from -6 to 6
Outputs:
- block_out: bfloat16 [2048, 1024], P('dp', 'col')
- grad_hidden: float32 [2048, 1024], P('dp', 'col')
- grad_embed: float32 [2048, 1024], P('dp', 'col')
- grad_gain_attn: float32 [2, 1024], P(None, 'col')
- grad_qkv: float32 [3, 2, 1024, 2048], P(None, None, 'col', 'row')
- grad_attn_out: float32 [2048, 2, 1024], P('row', None, 'col')
- grad_gain_mlp: float32 [2, 1024], P(None, 'col')
- grad_gate_up: float32 [2, 2, 1024, 4096], P(None, None, 'col', 'row')
- grad_lora_down: float32 [2, 1024, 128], P(None, 'col')
- grad_lora_up: float32 [2, 128, 4096], P(None, None, ('row', 'col'))
- grad_down: float32 [4096, 2, 1024], P('row', None, 'col')
- grad_proj: float32 [2, 1024, 1024], P(None, 'col')
- grad_gain_mixer: float32 [1024], P('col')
- grad_in_zx: float32 [2, 1024, 2048], P(None, 'col', 'row')
- grad_in_bcdt: float32 [1024, 160], P('col')
- grad_conv_inner: float32 [4, 2048], P(None, ('row', 'col'))
- grad_conv_state: float32 [4, 128], replicated
- grad_step_bias: float32 [32], P(('row', 'col'))
- grad_decay_log: float32 [32], P(('row', 'col'))
- grad_skip_gain: float32 [32], P(('row', 'col'))
- grad_gain_gated: float32 [2048], P(('row', 'col'))
- grad_out_weight: float32 [2048, 1024], P('row', 'col')
Inputs may be any that keep to these rules, and one draw needn't show every extreme that they name: `document_numbers`: each sequence of 512 tokens holds exactly four documents: the id is 0 at the first token and rises by one exactly where document_start_flags is 1. `document_start_flags`: 1 at the first token of every sequence of 512 tokens and where document_numbers rises, four times in each sequence.
All inputs are finite; a program needn't handle non-finite values.
Results may differ from a plain program's by a relative error of at most 0.03.
Values may be sent and summed in bfloat16 or wider, within the bound.
A program may use at most 192 MiB of HBM per device.

v0:
```python
import functools
import math

import jax
import jax.numpy as jnp
from jax import lax
from jax.sharding import PartitionSpec as P

MODEL_WIDTH = 1024
CONCAT_WIDTH = 2048
HD = 128
DI = 2048


EPS = 1e-05
FULL_PRECISION = lax.Precision.HIGHEST


def matrix_product(left, right):
    return jnp.dot(left, right, preferred_element_type=jnp.float32)


def matmul_tn(left, right):
    return lax.dot_general(
        left, right, (((0,), (0,)), ((), ())), preferred_element_type=jnp.float32
    )


def matrix_product_transposed(left, right):
    return lax.dot_general(
        left, right, (((1,), (1,)), ((), ())), preferred_element_type=jnp.float32
    )


def exact_product(left, right):
    return jnp.dot(left, right, precision=FULL_PRECISION)


def rope_tables(length, width):
    half = width // 2
    positions = jnp.arange(length).astype(jnp.float32)
    rates = jnp.exp(-math.log(10000.0) * jnp.arange(half).astype(jnp.float32) / half)
    angles = positions[:, None] * rates[None, :]
    return (jnp.cos(angles)[:, None, :], jnp.sin(angles)[:, None, :])


def rotate(vectors, cosine, sine):
    half = vectors.shape[-1] // 2
    first = vectors[..., :half]
    second = vectors[..., half:]
    return jnp.concatenate([first * cosine - second * sine, first * sine + second * cosine], -1)


def attention_core(queries, keys, values, segment):
    length = queries.shape[0]
    width = queries.shape[2]
    cosine, sine = rope_tables(length, width)
    queries = rotate(queries, cosine, sine)
    keys = rotate(keys, cosine, sine)
    scores = jnp.einsum("qhd,khd->hqk", queries, keys, precision=FULL_PRECISION) / math.sqrt(width)
    places = jnp.arange(length)
    allowed = (places[:, None] >= places[None, :]) & (segment[:, None] == segment[None, :])
    weight_list = jnp.where(allowed[None], jnp.exp(scores), 0.0)
    weight_list = weight_list / jnp.sum(weight_list, -1, keepdims=True)
    return jnp.einsum("hqk,khd->qhd", weight_list, values, precision=FULL_PRECISION)


def conv_causal(signal, kernel, docs):
    total = signal * kernel[0]
    for offset in range(1, kernel.shape[0]):
        shifted = jnp.concatenate(
            [jnp.zeros((offset, signal.shape[1]), signal.dtype), signal[:-offset]], 0
        )
        shifted_docs = jnp.concatenate([jnp.full((offset,), -1, jnp.int32), docs[:-offset]], 0)
        same = (shifted_docs == docs).astype(signal.dtype)[:, None]
        total = total + shifted * kernel[offset] * same
    return total


def bc_activate(bc_pre, kernel, docs):
    return jax.nn.silu(conv_causal(bc_pre, kernel, docs))


def mixer_core(
    x_pre,
    gate_z,
    step_raw,
    bc_conv,
    conv_kernel,
    step_offset_bias,
    log_decay_rates,
    head_skip_term,
    docs,
):
    length = x_pre.shape[0]
    heads = step_raw.shape[1]
    head_dim = x_pre.shape[1] // heads
    state = bc_conv.shape[1] // 2
    inner = jax.nn.silu(conv_causal(x_pre, conv_kernel, docs)).reshape(length, heads, head_dim)
    b_states = bc_conv[:, :state]
    c_states = bc_conv[:, state:]
    step = jax.nn.softplus(step_raw + step_offset_bias)
    rate = -jnp.exp(log_decay_rates) * step
    cumulative = jnp.cumsum(rate, 0)
    places = jnp.arange(length)
    allowed = ((places[:, None] >= places[None, :]) & (docs[:, None] == docs[None, :]))[None]
    gaps = cumulative.T[:, :, None] - cumulative.T[:, None, :]
    decay = jnp.where(allowed, jnp.exp(jnp.where(allowed, gaps, 0.0)), 0.0)
    intersection = jnp.dot(c_states, b_states.T, precision=FULL_PRECISION)
    mixing = decay * intersection[None]
    weighted = inner * step[:, :, None]
    outputs = jnp.einsum("hts,shp->thp", mixing, weighted, precision=FULL_PRECISION)
    outputs = outputs + head_skip_term[None, :, None] * inner
    return outputs.reshape(length, heads * head_dim) * jax.nn.silu(gate_z)


def gelu_product(gate_preact, up_preact):
    return jax.nn.gelu(gate_preact, approximate=True) * up_preact


def column_sum_total(values):
    return lax.psum(values, "col")


def overall_total(values):
    return lax.psum(values, ("row", "col"))


def row_total(values):
    return lax.psum(values, "row")


def owner_split(values):
    return lax.psum_scatter(values, "col", scatter_dimension=2, tiled=True)


def owner_join(values):
    return lax.all_gather(values, "col", axis=2, tiled=True)


def stream_norm(values, count):
    total = column_sum_total(jnp.sum(values * values, 1))
    scale = lax.rsqrt(total / count + EPS)[:, None]
    return (values * scale, scale)


def stream_norm_back(grad_in, normal, scale, gain, count):
    grad_hat = grad_in * gain
    inner = column_sum_total(jnp.sum(grad_hat * normal, 1)) / count
    return (scale * (grad_hat - normal * inner[:, None]), jnp.sum(grad_in * normal, 0))


def body(
    hidden_state_input,
    initial_token_embedding,
    document_numbers,
    document_start_flags,
    attention_norm_gain,
    query_key_value_matrix,
    attention_out_matrix,
    perceptron_norm_gain,
    gate_up_matrix,
    adapter_down,
    adapter_up,
    down_matrix,
    projection_matrix,
    mixer_norm_gain,
    gate_in_matrix,
    state_in_matrix,
    mixer_input_kernel,
    state_conv_kernel,
    step_offset_bias,
    log_decay_rates,
    head_skip_term,
    gated_norm_gain,
    mixer_out_matrix,
    output_gradient,
):
    length = hidden_state_input.shape[0]
    local_width = 2 * hidden_state_input.shape[1]
    concat = (
        jnp.stack([hidden_state_input, initial_token_embedding], 1)
        .astype(jnp.float32)
        .reshape(length, local_width)
    )
    attn_gain = attention_norm_gain.reshape(local_width)
    mlp_gain = perceptron_norm_gain.reshape(local_width)
    qkv_flat = query_key_value_matrix.reshape(3, local_width, query_key_value_matrix.shape[3])
    attn_out_flat = attention_out_matrix.reshape(attention_out_matrix.shape[0], local_width)
    gate_up_rows = gate_up_matrix.reshape(2, local_width, gate_up_matrix.shape[3])
    adapter_down_rows = adapter_down.reshape(local_width, adapter_down.shape[2])
    adapter_up_broad = adapter_up.astype(jnp.float32)
    down_flat = down_matrix.reshape(down_matrix.shape[0], local_width)
    proj_flat = projection_matrix.reshape(local_width, projection_matrix.shape[2])
    norm_one, scale_one = stream_norm(concat, CONCAT_WIDTH)
    normed_one = (norm_one * attn_gain).astype(jnp.bfloat16)
    qkv_own = owner_split(
        jnp.einsum("tc,kch->kth", normed_one, qkv_flat, preferred_element_type=jnp.float32)
    )
    heads_here = qkv_own.shape[2] // HD
    queries = qkv_own[0].reshape(length, heads_here, HD)
    keys_pre = qkv_own[1].reshape(length, heads_here, HD)
    values_pre = qkv_own[2].reshape(length, heads_here, HD)
    attended = attention_core(queries, keys_pre, values_pre, document_numbers)
    heads_half = owner_join(attended.reshape(1, length, -1).astype(jnp.bfloat16))[0]
    attn_stream = concat + row_total(matrix_product(heads_half, attn_out_flat))
    norm_two, scale_two = stream_norm(attn_stream, CONCAT_WIDTH)
    second_normed = (norm_two * mlp_gain).astype(jnp.bfloat16)
    adapter_middle = column_sum_total(matrix_product(second_normed, adapter_down_rows))
    gate_up_local = owner_split(
        jnp.einsum("tc,kcf->ktf", second_normed, gate_up_rows, preferred_element_type=jnp.float32)
    )
    gate_up_local = gate_up_local + jnp.einsum(
        "gb,sbm->sgm", adapter_middle, adapter_up_broad, precision=FULL_PRECISION
    )
    hidden_own = gelu_product(gate_up_local[0], gate_up_local[1]).astype(jnp.bfloat16)
    hidden_half = owner_join(hidden_own[None])[0]
    mixed = attn_stream + row_total(matrix_product(hidden_half, down_flat))
    mixed_b = mixed.astype(jnp.bfloat16)
    resid = (
        hidden_state_input.astype(jnp.float32)
        + owner_split(matrix_product(mixed_b, proj_flat)[None])[0]
    )
    norm_three, scale_three = stream_norm(resid, MODEL_WIDTH)
    normed_three = (norm_three * mixer_norm_gain).astype(jnp.bfloat16)
    zx_own = owner_split(
        jnp.einsum("tc,kci->kti", normed_three, gate_in_matrix, preferred_element_type=jnp.float32)
    )
    bcdt = column_sum_total(matrix_product(normed_three, state_in_matrix))
    state_cols = state_conv_kernel.shape[1]
    heads_own = step_offset_bias.shape[0]
    owner = lax.axis_index("row") * lax.axis_size("col") + lax.axis_index("col")
    step_own = lax.dynamic_slice_in_dim(bcdt, state_cols + owner * heads_own, heads_own, 1)
    docs = jnp.cumsum(document_start_flags) - 1
    bc_conv = bc_activate(bcdt[:, :state_cols], state_conv_kernel, docs)
    gated = mixer_core(
        zx_own[1],
        zx_own[0],
        step_own,
        bc_conv,
        mixer_input_kernel,
        step_offset_bias,
        log_decay_rates,
        head_skip_term,
        docs,
    )
    mean_square = overall_total(jnp.sum(gated * gated, 1)) / DI
    scale_four = lax.rsqrt(mean_square + EPS)[:, None]
    norm_four = gated * scale_four
    normed_own = (norm_four * gated_norm_gain).astype(jnp.bfloat16)
    normed_half = owner_join(normed_own[None])[0]
    output = resid + row_total(matrix_product(normed_half, mixer_out_matrix))
    block_out = output.astype(jnp.bfloat16)
    grad_top = output_gradient.astype(jnp.float32)
    grad_mixer_out_matrix = matmul_tn(normed_half, output_gradient)
    d_normed_four = owner_split(matrix_product_transposed(output_gradient, mixer_out_matrix)[None])[
        0
    ]
    grad_hat = d_normed_four * gated_norm_gain
    inner_four = overall_total(jnp.sum(grad_hat * norm_four, 1)) / DI
    d_gated = scale_four * (grad_hat - norm_four * inner_four[:, None])
    grad_gated_gain = jnp.sum(d_normed_four * norm_four, 0)
    core_back = jax.vjp(
        functools.partial(mixer_core, docs=docs),
        zx_own[1],
        zx_own[0],
        step_own,
        bc_conv,
        mixer_input_kernel,
        step_offset_bias,
        log_decay_rates,
        head_skip_term,
    )[1]
    (
        d_x_pre,
        d_gate_z,
        d_step_own,
        d_bc_part,
        grad_mixer_input_kernel,
        grad_step_offset_bias,
        grad_log_decay,
        grad_head_skip,
    ) = core_back(d_gated)
    step_slot = lax.dynamic_update_slice_in_dim(
        jnp.zeros((length, bcdt.shape[1] - state_cols), jnp.float32),
        d_step_own,
        owner * heads_own,
        1,
    )
    d_bcdt_sum = overall_total(jnp.concatenate([d_bc_part, step_slot], 1))
    bc_back = jax.vjp(
        functools.partial(bc_activate, docs=docs), bcdt[:, :state_cols], state_conv_kernel
    )[1]
    d_bc_pre, grad_state_conv_kernel = bc_back(d_bcdt_sum[:, :state_cols])
    d_bcdt_b = jnp.concatenate([d_bc_pre, d_bcdt_sum[:, state_cols:]], 1).astype(jnp.bfloat16)
    d_zx_half = owner_join(jnp.stack([d_gate_z, d_x_pre]).astype(jnp.bfloat16))
    grad_gate_in_matrix = jnp.einsum(
        "tc,kti->kci", normed_three, d_zx_half, preferred_element_type=jnp.float32
    )
    grad_state_in_matrix = matmul_tn(normed_three, d_bcdt_b)
    d_normed_three = row_total(
        jnp.einsum("kti,kci->tc", d_zx_half, gate_in_matrix, preferred_element_type=jnp.float32)
    )
    d_normed_three = d_normed_three + matrix_product_transposed(d_bcdt_b, state_in_matrix)
    d_norm_three, grad_mixer_gain = stream_norm_back(
        d_normed_three, norm_three, scale_three, mixer_norm_gain, MODEL_WIDTH
    )
    d_resid = grad_top + d_norm_three
    d_resid_full = owner_join(d_resid.astype(jnp.bfloat16)[None])[0]
    grad_projection_matrix = matmul_tn(mixed_b, d_resid_full).reshape(projection_matrix.shape)
    d_mixed = matrix_product_transposed(d_resid_full, proj_flat)
    d_mixed_b = d_mixed.astype(jnp.bfloat16)
    grad_down_matrix = matmul_tn(hidden_half, d_mixed_b).reshape(down_matrix.shape)
    d_hidden_own = owner_split(matrix_product_transposed(d_mixed_b, down_flat)[None])[0]
    act_back = jax.vjp(gelu_product, gate_up_local[0], gate_up_local[1])[1]
    grad_gate_preact, grad_up_preact = act_back(d_hidden_own)
    grad_gate_up_local = jnp.stack([grad_gate_preact, grad_up_preact])
    grad_adapter_up = jnp.einsum(
        "mc,ymv->ycv", adapter_middle, grad_gate_up_local, precision=FULL_PRECISION
    )
    grad_adapter_middle = overall_total(
        jnp.einsum("oaj,opj->ap", grad_gate_up_local, adapter_up_broad, precision=FULL_PRECISION)
    )
    d_gate_up_half = owner_join(grad_gate_up_local.astype(jnp.bfloat16))
    grad_gate_up_matrix = jnp.einsum(
        "tc,ktf->kcf", second_normed, d_gate_up_half, preferred_element_type=jnp.float32
    ).reshape(gate_up_matrix.shape)
    grad_second_normed = row_total(
        jnp.einsum("ktf,kcf->tc", d_gate_up_half, gate_up_rows, preferred_element_type=jnp.float32)
    )
    grad_second_normed = grad_second_normed + exact_product(
        grad_adapter_middle, adapter_down_rows.astype(jnp.float32).T
    )
    grad_adapter_down = exact_product(
        second_normed.astype(jnp.float32).T, grad_adapter_middle
    ).reshape(adapter_down.shape)
    d_norm_two, grad_perceptron_gain = stream_norm_back(
        grad_second_normed, norm_two, scale_two, mlp_gain, CONCAT_WIDTH
    )
    d_attn = d_mixed + d_norm_two
    d_attn_b = d_attn.astype(jnp.bfloat16)
    grad_attention_out = matmul_tn(heads_half, d_attn_b).reshape(attention_out_matrix.shape)
    d_heads_own = owner_split(matrix_product_transposed(d_attn_b, attn_out_flat)[None])[0]
    attn_back = jax.vjp(
        functools.partial(attention_core, segment=document_numbers), queries, keys_pre, values_pre
    )[1]
    d_queries, d_keys, d_values = attn_back(d_heads_own.reshape(length, heads_here, HD))
    d_qkv_half = owner_join(
        jnp.stack([d_queries, d_keys, d_values]).reshape(3, length, -1).astype(jnp.bfloat16)
    )
    grad_query_key_value = jnp.einsum(
        "tc,kth->kch", normed_one, d_qkv_half, preferred_element_type=jnp.float32
    ).reshape(query_key_value_matrix.shape)
    d_normed_one = row_total(
        jnp.einsum("kth,kch->tc", d_qkv_half, qkv_flat, preferred_element_type=jnp.float32)
    )
    d_norm_one, grad_attention_gain = stream_norm_back(
        d_normed_one, norm_one, scale_one, attn_gain, CONCAT_WIDTH
    )
    d_concat = (d_attn + d_norm_one).reshape(length, 2, hidden_state_input.shape[1])
    grad_hidden = d_resid + d_concat[:, 0]
    grad_embed = d_concat[:, 1]
    grad_attention_gain = grad_attention_gain.reshape(attention_norm_gain.shape)
    grad_perceptron_gain = grad_perceptron_gain.reshape(perceptron_norm_gain.shape)
    summed = lax.psum(
        (
            grad_attention_gain,
            grad_query_key_value,
            grad_attention_out,
            grad_perceptron_gain,
            grad_gate_up_matrix,
            grad_adapter_down,
            grad_adapter_up,
            grad_down_matrix,
            grad_projection_matrix,
            grad_mixer_gain,
            grad_gate_in_matrix,
            grad_state_in_matrix,
            grad_mixer_input_kernel,
            grad_state_conv_kernel,
            grad_step_offset_bias,
            grad_log_decay,
            grad_head_skip,
            grad_gated_gain,
            grad_mixer_out_matrix,
        ),
        "dp",
    )
    block_sums = tuple(summed[:8])
    mixer_sums = tuple(summed[8:])
    return (block_out, grad_hidden, grad_embed) + tuple(block_sums) + tuple(mixer_sums)


def solution(mesh):
    return jax.shard_map(
        body,
        mesh=mesh,
        in_specs=(
            P("dp", "col"),
            P("dp", "col"),
            P("dp"),
            P("dp"),
            P(None, "col"),
            P(None, None, "col", "row"),
            P("row", None, "col"),
            P(None, "col"),
            P(None, None, "col", "row"),
            P(None, "col", None),
            P(None, None, ("row", "col")),
            P("row", None, "col"),
            P(None, "col", None),
            P("col"),
            P(None, "col", "row"),
            P("col", None),
            P(None, ("row", "col")),
            P(),
            P(("row", "col")),
            P(("row", "col")),
            P(("row", "col")),
            P(("row", "col")),
            P("row", "col"),
            P("dp", "col"),
        ),
        out_specs=(
            P("dp", "col"),
            P("dp", "col"),
            P("dp", "col"),
            P(None, "col"),
            P(None, None, "col", "row"),
            P("row", None, "col"),
            P(None, "col"),
            P(None, None, "col", "row"),
            P(None, "col", None),
            P(None, None, ("row", "col")),
            P("row", None, "col"),
            P(None, "col", None),
            P("col"),
            P(None, "col", "row"),
            P("col", None),
            P(None, ("row", "col")),
            P(),
            P(("row", "col")),
            P(("row", "col")),
            P(("row", "col")),
            P(("row", "col")),
            P("row", "col"),
        ),
        check_vma=False,
    )
```

profile of v0, /device:TPU:0, one launch (start us, length us, event | category | flops | bytes accessed | tf_op | source)
XLA Modules:
  0.0 1919.6 jit_solution(1105299731079874820)
XLA Ops:
  31.1 105.8 %reduce-scatter.8.cloned.1.call-done = f32[3,512,256]{2,1,0:T(8,128)} async-done(((f32[3,512,1024]{2,1,0:T(8,128)}), f32[3,512,256]{2,1,0:T(8,128)}) %reduce-scatter.8.cloned.1.call-update) | async-done | bytes 1572880 | tf_op jit(solution)/shard_map/reduce_scatter | solution.py:134
  157.0 26.2 %all-gather.9.cloned.1.call-done = bf16[1,512,1024]{1,2,0:T(8,128)(2,1)} async-done(((bf16[1,512,256]{1,2,0:T(8,128)(2,1)}), bf16[1,512,1024]{1,2,0:T(8,128)(2,1)}) %all-gather.9.cloned.1.call-update) | async-done | bytes 1048592 | tf_op jit(solution)/shard_map/all_gather | solution.py:138
  188.7 16.7 all-reduce.42.cloned.1.call-done
  231.7 25.2 %all-reduce.44.cloned.1.call-done = f32[512,128]{1,0:T(8,128)} async-done(((f32[512,128]{1,0:T(8,128)}), f32[512,128]{1,0:T(8,128)}) %all-reduce.44.cloned.1.call-update) | async-done | bytes 262160 | tf_op jit(solution)/shard_map/psum | solution.py:122
  256.9 147.3 %reduce-scatter.10.cloned.1.call-done = f32[2,512,512]{2,1,0:T(8,128)} async-done(((f32[2,512,2048]{2,1,0:T(8,128)}), f32[2,512,512]{2,1,0:T(8,128)}) %reduce-scatter.10.cloned.1.call-update) | async-done | bytes 2097168 | tf_op jit(solution)/shard_map/reduce_scatter | solution.py:134
  412.9 43.0 %all-gather.11.cloned.1.call-done = bf16[1,512,2048]{2,1,0:T(8,128)(2,1)} async-done(((bf16[1,512,512]{2,1,0:T(8,128)(2,1)}), bf16[1,512,2048]{2,1,0:T(8,128)(2,1)}) %all-gather.11.cloned.1.call-update) | async-done | bytes 2097168 | tf_op jit(solution)/shard_map/all_gather | solution.py:138
  460.4 18.3 all-reduce.46.cloned.1.call-done
  486.4 41.9 %reduce-scatter.12.cloned.1.call-done = f32[1,512,256]{2,1,0:T(8,128)} async-done(((f32[1,512,1024]{2,1,0:T(8,128)}), f32[1,512,256]{2,1,0:T(8,128)}) %reduce-scatter.12.cloned.1.call-update) | async-done | bytes 524304 | tf_op jit(solution)/shard_map/reduce_scatter | solution.py:134
  551.2 22.9 %reduce-scatter.16.cloned.1.call-done = f32[1,512,256]{2,1,0:T(8,128)} async-done(((f32[1,512,1024]{2,1,0:T(8,128)}), f32[1,512,256]{2,1,0:T(8,128)}) %reduce-scatter.16.cloned.1.call-update) | async-done | bytes 524304 | tf_op jit(solution)/shard_map/reduce_scatter | solution.py:134
  576.1 36.2 %all-reduce.48.cloned.1.call-done = f32[512,160]{0,1:T(8,128)} async-done(((f32[512,160]{0,1:T(8,128)}), f32[512,160]{0,1:T(8,128)}) %all-reduce.48.cloned.1.call-update) | async-done | bytes 327696 | tf_op jit(solution)/shard_map/psum | solution.py:122
  622.8 69.0 %reduce-scatter.14.cloned.1.call-done = f32[2,512,256]{2,1,0:T(8,128)} async-done(((f32[2,512,1024]{2,1,0:T(8,128)}), f32[2,512,256]{2,1,0:T(8,128)}) %reduce-scatter.14.cloned.1.call-update) | async-done | bytes 1048592 | tf_op jit(solution)/shard_map/reduce_scatter | solution.py:134
  708.9 16.0 psum.266
  729.2 22.8 %psum.268 = f32[512]{0:T(512)S(1)} all-reduce(f32[512]{0:T(512)S(1)} %get-tuple-element.70), channel_id=1, replica_groups=mesh['dp'=4,'row'=2,'col'=4] {'row','col'}, use_global_device_ids=true, to_apply=%region_24.25 | all-reduce | flops 512 | bytes 4096 | tf_op jit(solution)/shard_map/psum | solution.py:126
  797.7 50.4 %all-reduce.52.cloned.1.call-done = f32[512,160]{0,1:T(8,128)} async-done(((f32[512,160]{0,1:T(8,128)}), f32[512,160]{0,1:T(8,128)}) %all-reduce.52.cloned.1.call-update) | async-done | bytes 327696 | tf_op jit(solution)/shard_map/psum | solution.py:126
  853.3 42.2 %all-gather.15.cloned.1.call-done = bf16[2,512,1024]{2,1,0:T(8,128)(2,1)} async-done(((bf16[2,512,256]{2,1,0:T(8,128)(2,1)}), bf16[2,512,1024]{2,1,0:T(8,128)(2,1)}) %all-gather.15.cloned.1.call-update) | async-done | bytes 2097168 | tf_op jit(solution)/shard_map/all_gather | solution.py:138
  934.3 28.2 %all-gather.21.cloned.1.call-done = bf16[512,1024]{1,0:T(8,128)(2,1)} async-done(((bf16[512,256]{1,0:T(8,128)(2,1)}), bf16[512,1024]{1,0:T(8,128)(2,1)}) %all-gather.21.cloned.1.call-update) | async-done | bytes 1048592 | tf_op jit(solution)/shard_map/all_gather | solution.py:138
  970.1 75.2 %reduce-scatter.18.cloned.1.call-done = f32[1,512,512]{2,1,0:T(8,128)} async-done(((f32[1,512,2048]{2,1,0:T(8,128)}), f32[1,512,512]{2,1,0:T(8,128)}) %reduce-scatter.18.cloned.1.call-update) | async-done | bytes 1048592 | tf_op jit(solution)/shard_map/reduce_scatter | solution.py:134
  1053.9 77.9 %all-gather.17.cloned.1.call-done = bf16[2,512,2048]{2,1,0:T(8,128)(2,1)} async-done(((bf16[2,512,512]{2,1,0:T(8,128)(2,1)}), bf16[2,512,2048]{2,1,0:T(8,128)(2,1)}) %all-gather.17.cloned.1.call-update) | async-done | bytes 4194320 | tf_op jit(solution)/shard_map/all_gather | solution.py:138
  1141.2 47.3 %all-reduce.56.cloned.1.call-done = f32[512,128]{1,0:T(8,128)} async-done(((f32[512,128]{1,0:T(8,128)}), f32[512,128]{1,0:T(8,128)}) %all-reduce.56.cloned.1.call-update) | async-done | bytes 262160 | tf_op jit(solution)/shard_map/psum | solution.py:126
  1188.5 21.4 %all-reduce.54.cloned.1.call-done = f32[512,512]{1,0:T(8,128)} async-done(((f32[512,512]{1,0:T(8,128)}), f32[512,512]{1,0:T(8,128)}) %all-reduce.54.cloned.1.call-update) | async-done | bytes 1048592 | tf_op jit(solution)/shard_map/psum | solution.py:130
  1234.6 40.7 %reduce-scatter.20.cloned.1.call-done = f32[1,512,256]{2,1,0:T(8,128)} async-done(((f32[1,512,1024]{2,1,0:T(8,128)}), f32[1,512,256]{2,1,0:T(8,128)}) %reduce-scatter.20.cloned.1.call-update) | async-done | bytes 524304 | tf_op jit(solution)/shard_map/reduce_scatter | solution.py:134
  1329.2 43.0 %all-gather.19.cloned.1.call-done = bf16[3,512,1024]{2,1,0:T(8,128)(2,1)} async-done(((bf16[3,512,256]{2,1,0:T(8,128)(2,1)}), bf16[3,512,1024]{2,1,0:T(8,128)(2,1)}) %all-gather.19.cloned.1.call-update) | async-done | bytes 3145744 | tf_op jit(solution)/shard_map/all_gather | solution.py:138
  1422.7 17.4 all-reduce.28
  1442.6 437.4 %all-reduce.58.cloned.1.call-done = (f32[3,2,256,1024]{3,2,1,0:T(8,128)}, f32[1024,2,256]{2,0,1:T(8,128)}, f32[2,2,256,2048]{3,2,1,0:T(8,128)}, f32[2,256,128]{2...) async-done(((f32[3,2,256,1024]{3,2,1,0:T(8,128)}, ...) | async-done | bytes 27164688 | tf_op jit(solution)/shard_map/psum | solution.py:365
  (512 shorter events, 431.3 us)
Async XLA Ops:
  7.2 129.7 %reduce-scatter.8.cloned.1.call-start = ((), (), s32[]{:S(2)}) async-start(), calls=%async_computation.7 | async-start | bytes 7864320 | tf_op jit(solution)/shard_map/reduce_scatter | solution.py:134
  27.7 155.4 %all-gather.9.cloned.1.call-start = ((), (), s32[]{:S(2)}) async-start(), calls=%async_computation.8 | async-start | bytes 1310720 | tf_op jit(solution)/shard_map/all_gather | solution.py:138
  154.5 50.9 %all-reduce.42.cloned.1.call-start = ((), (), s32[]{:S(2)}) async-start(), calls=%async_computation.9 | async-start | bytes 2097152 | tf_op jit(solution)/shard_map/psum | solution.py:130
  186.5 70.5 %all-reduce.44.cloned.1.call-start = ((), (), s32[]{:S(2)}) async-start(), calls=%async_computation.11 | async-start | bytes 524288 | tf_op jit(solution)/shard_map/psum | solution.py:122
  223.2 181.0 %reduce-scatter.10.cloned.1.call-start = ((), (), s32[]{:S(2)}) async-start(), calls=%async_computation.10 | async-start | bytes 10485760 | tf_op jit(solution)/shard_map/reduce_scatter | solution.py:134
  231.7 224.2 %all-gather.11.cloned.1.call-start = ((), (), s32[]{:S(2)}) async-start(), calls=%async_computation.12 | async-start | bytes 2621440 | tf_op jit(solution)/shard_map/all_gather | solution.py:138
  409.4 69.3 %all-reduce.46.cloned.1.call-start = ((), (), s32[]{:S(2)}) async-start(), calls=%async_computation.13 | async-start | bytes 2097152 | tf_op jit(solution)/shard_map/psum | solution.py:130
  460.3 68.0 %reduce-scatter.12.cloned.1.call-start = ((), (), s32[]{:S(2)}) async-start(), calls=%async_computation.14 | async-start | bytes 2621440 | tf_op jit(solution)/shard_map/reduce_scatter | solution.py:134
  483.4 90.7 %reduce-scatter.16.cloned.1.call-start = ((), (), s32[]{:S(2)}) async-start(), calls=%async_computation.18 | async-start | bytes 2621440 | tf_op jit(solution)/shard_map/reduce_scatter | solution.py:134
  486.4 125.9 %all-reduce.48.cloned.1.call-start = ((), (), s32[]{:S(2)}) async-start(), calls=%async_computation.16 | async-start | bytes 655360 | tf_op jit(solution)/shard_map/psum | solution.py:122
  542.7 149.1 %reduce-scatter.14.cloned.1.call-start = ((), (), s32[]{:S(2)}) async-start(), calls=%async_computation.15 | async-start | bytes 5242880 | tf_op jit(solution)/shard_map/reduce_scatter | solution.py:134
  546.8 301.3 %all-reduce.52.cloned.1.call-start = ((), (), s32[]{:S(2)}) async-start(), calls=%async_computation.21 | async-start | bytes 655360 | tf_op jit(solution)/shard_map/psum | solution.py:126
  792.0 103.5 %all-gather.15.cloned.1.call-start = ((), (), s32[]{:S(2)}) async-start(), calls=%async_computation.19 | async-start | bytes 2621440 | tf_op jit(solution)/shard_map/all_gather | solution.py:138
  797.4 118.5 %all-reduce.50.cloned.1.call-start = ((), (), s32[]{:S(2)}) async-start(), calls=%async_computation.20 | async-start | bytes 1048576 | tf_op jit(solution)/shard_map/psum | solution.py:130
  899.0 63.6 %all-gather.21.cloned.1.call-start = ((), (), s32[]{:S(2)}) async-start(), calls=%async_computation.28 | async-start | bytes 1310720 | tf_op jit(solution)/shard_map/all_gather | solution.py:138
  934.3 111.0 %reduce-scatter.18.cloned.1.call-start = ((), (), s32[]{:S(2)}) async-start(), calls=%async_computation.22 | async-start | bytes 5242880 | tf_op jit(solution)/shard_map/reduce_scatter | solution.py:134
  970.1 161.8 %all-gather.17.cloned.1.call-start = ((), (), s32[]{:S(2)}) async-start(), calls=%async_computation.23 | async-start | bytes 5242880 | tf_op jit(solution)/shard_map/all_gather | solution.py:138
  1050.4 138.1 %all-reduce.56.cloned.1.call-start = ((), (), s32[]{:S(2)}) async-start(), calls=%async_computation.25 | async-start | bytes 524288 | tf_op jit(solution)/shard_map/psum | solution.py:126
  1053.9 156.1 %all-reduce.54.cloned.1.call-start = ((), (), s32[]{:S(2)}) async-start(), calls=%async_computation.24 | async-start | bytes 2097152 | tf_op jit(solution)/shard_map/psum | solution.py:130
  1138.7 136.7 %reduce-scatter.20.cloned.1.call-start = ((), (), s32[]{:S(2)}) async-start(), calls=%async_computation.26 | async-start | bytes 2621440 | tf_op jit(solution)/shard_map/reduce_scatter | solution.py:134
  1233.4 79.7 %all-gather.13.cloned.1.call-start = ((), (), s32[]{:S(2)}) async-start(), calls=%async_computation.17 | async-start | bytes 1310720 | tf_op jit(solution)/shard_map/all_gather | solution.py:138
  1234.1 138.0 %all-gather.19.cloned.1.call-start = ((), (), s32[]{:S(2)}) async-start(), calls=%async_computation.27 | async-start | bytes 3932160 | tf_op jit(solution)/shard_map/all_gather | solution.py:138
  1309.4 92.2 %all-reduce.60.cloned.1.call-start = ((), (), s32[]{:S(2)}) async-start(), calls=%async_computation.30 | async-start | bytes 3145728 | tf_op jit(solution)/shard_map/psum | solution.py:130
  1376.9 503.2 %all-reduce.58.cloned.1.call-start = ((), (), s32[]{:S(2)}) async-start(), calls=%async_computation.29 | async-start | bytes 54329344 | tf_op jit(solution)/shard_map/psum | solution.py:365
  (139 other events, 2831.1 us)
Sparse Core Ops, SparseCore 0:
  27.9 108.9 reduce-scatter.7
  154.6 28.4 all-gather.8
  186.6 18.7 all-reduce.41
  223.4 33.5 all-reduce.43
  259.7 144.4 reduce-scatter.9
  409.6 46.2 all-gather.10
  460.5 18.2 all-reduce.45
  483.5 44.7 reduce-scatter.11
  531.2 42.8 reduce-scatter.15
  576.8 35.4 all-reduce.47
  615.2 76.5 reduce-scatter.13
  792.1 55.8 all-reduce.51
  850.2 45.2 all-gather.14
  899.1 16.7 all-reduce.49
  934.4 28.0 all-gather.20
  970.2 75.0 reduce-scatter.17
  1050.5 81.2 all-gather.16
  1134.6 53.9 all-reduce.55
  1191.4 18.4 all-reduce.53
  1233.5 41.7 reduce-scatter.19
  1276.9 29.0 all-gather.12
  1309.5 62.5 all-gather.18
  1377.0 18.5 all-reduce.59
  1402.0 477.9 all-reduce.57
where the time goes:
time: 1930 us; the launch traced here: 1920 us
  waiting for transfers between devices  1430 us (74%)
  matrix products  153 us (8%)
  blocking collectives  126 us (7%)
  local copies, waits for them, and re-layouts  112 us (6%)
  other arithmetic  82.1 us (4%)
    reduce_scatter x7, waiting for transfers between devices, owner_split(): return lax.psum_scatter(values, 'col', scatter_dimension=2, tiled=True)  503 us
    psum x1, waiting for transfers between devices, body(): lax.psum((grad_attention_gain, grad_query_key_value, grad_attention_out,...  437 us
    all_gather x7, waiting for transfers between devices, owner_join(): return lax.all_gather(values, 'col', axis=2, tiled=True)  260 us
    psum x2, waiting for transfers between devices, overall_total(): return lax.psum(values, ('row', 'col'))  97.6 us
    psum x6, blocking collectives, column_sum_total(): return lax.psum(values, 'col')  69.8 us
    psum x5, waiting for transfers between devices, row_total(): return lax.psum(values, 'row')  67.8 us
    psum x2, waiting for transfers between devices, column_sum_total(): return lax.psum(values, 'col')  61.3 us
    unnamed x294, local copies, waits for them, and re-layouts  50 us
  transfers between devices with their start and end apart: 24, of which 22 were waited for; matrix products, arithmetic and copies ran while one was open for 9% of the time, Pallas kernels for 0%

commit v1 on v0

v1 whole, which is shorter than its diff:
```python
import functools
import math

import jax
import jax.numpy as jnp
from jax import lax
from jax.experimental import pallas as pl
from jax.experimental.pallas import tpu as pltpu
from jax.sharding import PartitionSpec as P

EPS = 1e-05
FULL_PRECISION = lax.Precision.HIGHEST
BF = jnp.bfloat16
F32 = jnp.float32
MESH = pl.DeviceIdType.MESH


def matrix_product(left, right):
    return jnp.dot(left, right, preferred_element_type=F32)


def matmul_tn(left, right):
    return lax.dot_general(left, right, (((0,), (0,)), ((), ())), preferred_element_type=F32)


def matrix_product_transposed(left, right):
    return lax.dot_general(left, right, (((1,), (1,)), ((), ())), preferred_element_type=F32)


def rope_tables(length, width):
    half = width // 2
    positions = jnp.arange(length).astype(F32)
    rates = jnp.exp(-math.log(10000.0) * jnp.arange(half).astype(F32) / half)
    angles = positions[:, None] * rates[None, :]
    return (jnp.cos(angles)[:, None, :], jnp.sin(angles)[:, None, :])


def rotate(vectors, cosine, sine):
    half = vectors.shape[-1] // 2
    first = vectors[..., :half]
    second = vectors[..., half:]
    return jnp.concatenate([first * cosine - second * sine, first * sine + second * cosine], -1)


def attention_core(queries, keys, values, segment):
    length = queries.shape[0]
    width = queries.shape[2]
    cosine, sine = rope_tables(length, width)
    queries = rotate(queries, cosine, sine)
    keys = rotate(keys, cosine, sine)
    scores = jnp.einsum("qhd,khd->hqk", queries, keys, precision=FULL_PRECISION) / math.sqrt(width)
    places = jnp.arange(length)
    allowed = (places[:, None] >= places[None, :]) & (segment[:, None] == segment[None, :])
    weight_list = jnp.where(allowed[None], jnp.exp(scores), 0.0)
    weight_list = weight_list / jnp.sum(weight_list, -1, keepdims=True)
    return jnp.einsum("hqk,khd->qhd", weight_list, values, precision=FULL_PRECISION)


def conv_causal(signal, kernel, docs):
    total = signal * kernel[0]
    for offset in range(1, kernel.shape[0]):
        shifted = jnp.concatenate(
            [jnp.zeros((offset, signal.shape[1]), signal.dtype), signal[:-offset]], 0
        )
        shifted_docs = jnp.concatenate([jnp.full((offset,), -1, jnp.int32), docs[:-offset]], 0)
        same = (shifted_docs == docs).astype(signal.dtype)[:, None]
        total = total + shifted * kernel[offset] * same
    return total


def bc_activate(bc_pre, kernel, docs):
    return jax.nn.silu(conv_causal(bc_pre, kernel, docs))


def mixer_core(
    x_pre,
    gate_z,
    step_raw,
    bc_conv,
    conv_kernel,
    step_offset_bias,
    log_decay_rates,
    head_skip_term,
    docs,
):
    length = x_pre.shape[0]
    heads = step_raw.shape[1]
    head_dim = x_pre.shape[1] // heads
    state = bc_conv.shape[1] // 2
    inner = jax.nn.silu(conv_causal(x_pre, conv_kernel, docs)).reshape(length, heads, head_dim)
    b_states = bc_conv[:, :state]
    c_states = bc_conv[:, state:]
    step = jax.nn.softplus(step_raw + step_offset_bias)
    rate = -jnp.exp(log_decay_rates) * step
    cumulative = jnp.cumsum(rate, 0)
    places = jnp.arange(length)
    allowed = ((places[:, None] >= places[None, :]) & (docs[:, None] == docs[None, :]))[None]
    gaps = cumulative.T[:, :, None] - cumulative.T[:, None, :]
    decay = jnp.where(allowed, jnp.exp(jnp.where(allowed, gaps, 0.0)), 0.0)
    intersection = jnp.dot(c_states, b_states.T, precision=FULL_PRECISION)
    mixing = decay * intersection[None]
    weighted = inner * step[:, :, None]
    outputs = jnp.einsum("hts,shp->thp", mixing, weighted, precision=FULL_PRECISION)
    outputs = outputs + head_skip_term[None, :, None] * inner
    return outputs.reshape(length, heads * head_dim) * jax.nn.silu(gate_z)


def gelu_product(gate_preact, up_preact):
    return jax.nn.gelu(gate_preact, approximate=True) * up_preact


def _window(index, size):
    return pl.ds(pl.multiple_of(index * size, size), size)


def _add_rows(rows, write):
    chunk = 64 if rows % 64 == 0 else rows
    if rows == chunk:
        write(pl.ds(0, rows))
        return

    def step(i, carry):
        write(pl.ds(pl.multiple_of(i * chunk, chunk), chunk))
        return carry

    lax.fori_loop(0, rows // chunk, step, 0)


def _remote(src, dst, send, recv, device):
    copy = pltpu.make_async_remote_copy(
        src_ref=src,
        dst_ref=dst,
        send_sem=send,
        recv_sem=recv,
        device_id=device,
        device_id_type=MESH,
    )
    copy.start()
    return copy


class Env:
    def __init__(self, n):
        self.n = n
        self.col = lax.axis_index("col")
        self.row = lax.axis_index("row")
        self.sibling = {"row": 1 - self.row}

    def peer(self, k):
        return {"col": lax.rem(self.col + k, self.n)}


def run_gather(env, x, o, send, recv, local):
    width = x.shape[1]
    here = o.at[:, _window(env.col, width)]
    copies = [
        _remote(x, here, send.at[k - 1], recv.at[k - 1], env.peer(k)) for k in range(1, env.n)
    ]
    own = pltpu.make_async_copy(x, here, local.at[0])
    own.start()
    yield
    own.wait()
    for copy in copies:
        copy.wait()


def run_gather2(env, x, o, send, recv, local, send2, recv2):
    width = x.shape[1]
    half = x.shape[0] // 2
    mine = _window(env.row, half)
    copies = [
        _remote(
            x.at[mine, :],
            o.at[mine, _window(env.col, width)],
            send.at[k - 1],
            recv.at[k - 1],
            env.peer(k),
        )
        for k in range(1, env.n)
    ]
    own = pltpu.make_async_copy(x, o.at[:, _window(env.col, width)], local.at[0])
    own.start()
    yield
    onward = []
    for k in range(1, env.n):
        copies[k - 1].wait()
        part = o.at[mine, _window(lax.rem(env.col + env.n - k, env.n), width)]
        onward.append(_remote(part, part, send2.at[k - 1], recv2.at[k - 1], env.sibling))
    yield
    own.wait()
    for copy in onward:
        copy.wait()


def run_scatter(env, p, o, buffer, send, recv):
    rows, width = o.shape
    copies = [
        _remote(
            p.at[:, _window(lax.rem(env.col + k, env.n), width)],
            buffer.at[k - 1],
            send.at[k - 1],
            recv.at[k - 1],
            env.peer(k),
        )
        for k in range(1, env.n)
    ]
    yield
    for copy in copies:
        copy.wait()

    def write(part):
        total = p[part, _window(env.col, width)].astype(F32)
        for k in range(env.n - 1):
            total = total + buffer[k, part, :].astype(F32)
        o[part, :] = total

    _add_rows(rows, write)


def run_scatter2(env, p, o, buffer, send, recv, send2, recv2):
    rows, width = p.shape[0], o.shape[1]
    copies = [
        _remote(
            p.at[:, _window(lax.rem(env.col + k, env.n), width)],
            buffer.at[k - 1],
            send.at[k - 1],
            recv.at[k - 1],
            env.peer(k),
        )
        for k in range(1, env.n)
    ]
    yield
    for copy in copies:
        copy.wait()
    first = env.row * rows

    def write(part):
        total = p[part, _window(env.col, width)].astype(F32)
        for k in range(env.n - 1):
            total = total + buffer[k, part, :].astype(F32)
        target = pl.ds(pl.multiple_of(first + part.start, 8), part.size)
        o[target, :] = total

    _add_rows(rows, write)
    half = o.at[_window(env.row, rows), :]
    copy = _remote(half, half, send2.at[0], recv2.at[0], env.sibling)
    yield
    copy.wait()


def run_reduce(env, p, o, pairs, sums, buffer, send, recv, send2, recv2, send3, recv3):
    rows, width = o.shape
    half = rows // 2
    mine, other = _window(env.row, half), _window(1 - env.row, half)
    order = [(k + 1) % env.n for k in range(env.n)]
    first = []
    for i, k in enumerate(order):
        piece = _window(lax.rem(env.col + k, env.n), width)
        first.append(
            _remote(p.at[other, piece], pairs.at[i], send.at[i], recv.at[i], env.sibling)
        )
    yield
    start = env.row * half
    copies = []
    for i, k in enumerate(order):
        first[i].wait()
        piece = _window(lax.rem(env.col + k, env.n), width)

        def write(part, i=i, piece=piece, k=k):
            source = pl.ds(pl.multiple_of(start + part.start, 16), part.size)
            total = p[source, piece].astype(F32) + pairs[i, part, :].astype(F32)
            sums[i, part, :] = total.astype(sums.dtype)

        _add_rows(half, write)
        if k:
            copies.append(
                _remote(sums.at[i], buffer.at[i], send2.at[i], recv2.at[i], env.peer(k))
            )
    yield
    for copy in copies:
        copy.wait()

    def finish(part):
        total = sums[env.n - 1, part, :].astype(F32)
        for k in range(env.n - 1):
            total = total + buffer[k, part, :].astype(F32)
        target = pl.ds(pl.multiple_of(start + part.start, 8), part.size)
        o[target, :] = total

    _add_rows(half, finish)
    part = o.at[mine, :]
    copy = _remote(part, part, send3.at[0], recv3.at[0], env.sibling)
    yield
    copy.wait()


def run_a2a(env, x, o, send, recv, local):
    width = o.shape[2]
    copies = [
        _remote(
            x.at[:, _window(lax.rem(env.col + k, env.n), width)],
            o.at[env.col],
            send.at[k - 1],
            recv.at[k - 1],
            env.peer(k),
        )
        for k in range(1, env.n)
    ]
    own = pltpu.make_async_copy(x.at[:, _window(env.col, width)], o.at[env.col], local.at[0])
    own.start()
    yield
    own.wait()
    for copy in copies:
        copy.wait()


def run_a2a_back(env, x, o, send, recv, local):
    width = x.shape[2]
    here = o.at[:, _window(env.col, width)]
    copies = [
        _remote(x.at[lax.rem(env.col + k, env.n)], here, send.at[k - 1], recv.at[k - 1], env.peer(k))
        for k in range(1, env.n)
    ]
    own = pltpu.make_async_copy(x.at[env.col], here, local.at[0])
    own.start()
    yield
    own.wait()
    for copy in copies:
        copy.wait()


def run_rowsum(env, p, o, buffer, send, recv):
    copy = _remote(p, buffer, send.at[0], recv.at[0], env.sibling)
    yield
    copy.wait()

    def write(part):
        o[part, :] = p[part, :].astype(F32) + buffer[part, :].astype(F32)

    _add_rows(p.shape[0], write)


def run_sum(env, s, o, buffer, send, recv, local):
    both = buffer.shape[0] > env.n
    mine = env.row * env.n + env.col if both else env.col
    copies = []
    for r in range(2 if both else 1):
        for k in range(env.n):
            if r == 0 and k == 0:
                continue
            device = dict(env.peer(k)) if k else {}
            if r:
                device["row"] = 1 - env.row
            index = r * env.n + k - 1
            copies.append(_remote(s, buffer.at[mine], send.at[index], recv.at[index], device))
    own = pltpu.make_async_copy(s, buffer.at[mine], local.at[0])
    own.start()
    yield
    own.wait()
    for copy in copies:
        copy.wait()
    total = buffer[0]
    for i in range(1, buffer.shape[0]):
        total = total + buffer[i]
    o[...] = total


def plan(kind, x, n):
    dma = pltpu.SemaphoreType.DMA
    shape = x.shape
    three = dma((n - 1,))
    one = dma((1,))
    if kind == "gather":
        return run_gather, (shape[0], n * shape[1]), x.dtype, [three, three, one]
    if kind == "gather2":
        return run_gather2, (shape[0], n * shape[1]), x.dtype, [three, three, one, three, three]
    if kind == "scatter":
        out = (shape[0], shape[1] // n)
        return run_scatter, out, F32, [pltpu.VMEM((n - 1,) + out, x.dtype), three, three]
    if kind == "scatter2":
        part = (shape[0], shape[1] // n)
        out = (2 * shape[0], shape[1] // n)
        scratch = [pltpu.VMEM((n - 1,) + part, x.dtype), three, three, one, one]
        return run_scatter2, out, F32, scratch
    if kind == "reduce":
        out = (shape[0], shape[1] // n)
        part = (shape[0] // 2, shape[1] // n)
        four = dma((n,))
        scratch = [
            pltpu.VMEM((n,) + part, x.dtype),
            pltpu.VMEM((n,) + part, x.dtype),
            pltpu.VMEM((n - 1,) + part, x.dtype),
            four,
            four,
            three,
            three,
            one,
            one,
        ]
        return run_reduce, out, F32, scratch
    if kind == "a2a":
        return run_a2a, (n, shape[0], shape[1] // n), x.dtype, [three, three, one]
    if kind == "a2a_back":
        return run_a2a_back, (shape[1], n * shape[2]), x.dtype, [three, three, one]
    if kind == "rowsum":
        return run_rowsum, shape, F32, [pltpu.VMEM(shape, x.dtype), one, one]
    members = n if kind == "colsum" else 2 * n
    many = dma((members - 1,))
    return run_sum, shape, F32, [pltpu.VMEM((members,) + shape, x.dtype), many, many, one]


def exchange(ident, items, micros):
    n = lax.axis_size("col")
    plans = [plan(kind, x, n) for kind, x in items]
    kinds = {kind for kind, _ in items}
    count = len(items)
    use_all = "allsum" in kinds
    use_col = use_all or bool(kinds - {"rowsum"})
    use_row = use_all or bool(kinds & {"rowsum", "gather2", "scatter2", "reduce"})

    def kernel(*refs):
        env = Env(n)
        barrier = pltpu.get_barrier_semaphore()
        targets = []
        if use_col:
            targets += [env.peer(k) for k in range(1, n)]
        if use_row:
            targets.append(env.sibling)
        if use_all:
            targets += [{**env.peer(k), **env.sibling} for k in range(1, n)]
        for target in targets:
            pl.semaphore_signal(barrier, inc=1, device_id=target, device_id_type=MESH)
        pl.semaphore_wait(barrier, len(targets))
        position = 2 * count
        running = []
        for i in range(count):
            size = len(plans[i][3])
            scratch = refs[position : position + size]
            position += size
            running.append(plans[i][0](env, refs[i], refs[count + i], *scratch))
        while running:
            alive = []
            for item in running:
                try:
                    next(item)
                except StopIteration:
                    continue
                alive.append(item)
            running = alive

    vmem = pl.BlockSpec(memory_space=pltpu.VMEM)
    return pl.pallas_call(
        kernel,
        out_shape=[jax.ShapeDtypeStruct(p[1], p[2]) for p in plans],
        in_specs=[vmem] * count,
        out_specs=[vmem] * count,
        scratch_shapes=[s for p in plans for s in p[3]],
        compiler_params=pltpu.CompilerParams(collective_id=ident, has_side_effects=True),
        cost_estimate=pl.CostEstimate(
            flops=0, bytes_accessed=int(micros * 3000000), transcendentals=0
        ),
        name="exchange_%d" % ident,
    )(*[x for _, x in items])


def pack_rows(*vectors):
    return jnp.concatenate([v.reshape(-1, 128) for v in vectors], 0)


def unpack_rows(packed, count):
    return [part.reshape(-1) for part in jnp.split(packed, count, 0)]


def body(
    hidden_state_input,
    initial_token_embedding,
    document_numbers,
    document_start_flags,
    attention_norm_gain,
    query_key_value_matrix,
    attention_out_matrix,
    perceptron_norm_gain,
    gate_up_matrix,
    adapter_down,
    adapter_up,
    down_matrix,
    projection_matrix,
    mixer_norm_gain,
    gate_in_matrix,
    state_in_matrix,
    mixer_input_kernel,
    state_conv_kernel,
    step_offset_bias,
    log_decay_rates,
    head_skip_term,
    gated_norm_gain,
    mixer_out_matrix,
    output_gradient,
):
    n = lax.axis_size("col")
    replicas = lax.axis_size("dp")
    dp, row, col = lax.axis_index("dp"), lax.axis_index("row"), lax.axis_index("col")
    length, width = hidden_state_input.shape
    local_width = 2 * width
    model_width = n * width
    concat_width = n * local_width
    inner_width = gated_norm_gain.shape[0] * 2 * n

    def my_rows(weight):
        axis = weight.ndim - 2
        share = weight.shape[axis] // replicas
        part = lax.dynamic_slice_in_dim(weight, dp * share, share, axis)
        return part.reshape(-1, weight.shape[-1])

    def spread(pieces, lead):
        shaped = pieces.reshape(n, lead, -1, pieces.shape[2])
        return lax.all_gather(shaped, "dp", axis=2, tiled=True)

    def features_first(full, outer):
        inner = full.shape[1] // outer
        parts = full.reshape(n, outer, inner * full.shape[2], full.shape[3])
        return parts.transpose(1, 0, 2, 3).reshape(outer, -1, full.shape[3])

    attn_gain = attention_norm_gain.reshape(local_width)
    mlp_gain = perceptron_norm_gain.reshape(local_width)
    attn_out_flat = attention_out_matrix.reshape(attention_out_matrix.shape[0], local_width)
    down_flat = down_matrix.reshape(down_matrix.shape[0], local_width)
    proj_flat = projection_matrix.reshape(local_width, projection_matrix.shape[2])
    adapter_up_broad = adapter_up.astype(F32)
    state_width = state_in_matrix.shape[1]
    state_pad = jnp.pad(state_in_matrix, ((0, 0), (0, -state_width % 128)))

    (qkv_pieces,) = exchange(0, [("a2a", my_rows(query_key_value_matrix))], 20)
    qkv_t = features_first(spread(qkv_pieces, 6), 3)

    concat = (
        jnp.stack([hidden_state_input, initial_token_embedding], 1)
        .astype(F32)
        .reshape(length, local_width)
    )
    x_one, sum_one, gate_up_pieces, gate_in_pieces, adapter_down_full, state_full = exchange(
        1,
        [
            ("gather2", (concat * attn_gain).astype(BF)),
            ("colsum", pack_rows(jnp.sum(concat * concat, 1))),
            ("a2a", my_rows(gate_up_matrix)),
            ("a2a", my_rows(gate_in_matrix)),
            ("gather2", adapter_down.reshape(local_width, -1)),
            ("gather2", state_pad),
        ],
        60,
    )
    gate_up_t = features_first(spread(gate_up_pieces, 4), 2)
    gate_in_t = features_first(spread(gate_in_pieces, 2), 2)

    def stacked(gathered, lanes):
        rows = gathered.shape[0]
        return gathered.reshape(rows, n, lanes).transpose(1, 0, 2).reshape(n * rows, lanes)

    down_full = stacked(adapter_down_full, adapter_down.shape[2])
    state_in_full = stacked(state_full, state_pad.shape[1])[:, :state_width]

    d_normed_four = lax.psum_scatter(
        matrix_product_transposed(output_gradient, mixer_out_matrix).astype(BF)[None],
        "col",
        scatter_dimension=2,
        tiled=True,
    )[0].astype(F32)

    scale_one = lax.rsqrt(sum_one.reshape(-1) / concat_width + EPS)[:, None]
    norm_one = concat * scale_one
    normed_one = (x_one.astype(F32) * scale_one).astype(BF)
    head_size = 128
    qkv_own = jnp.einsum("tk,iko->ito", normed_one, qkv_t, preferred_element_type=F32)
    heads_here = qkv_own.shape[2] // head_size
    queries, keys_pre, values_pre = [
        qkv_own[i].reshape(length, heads_here, head_size) for i in range(3)
    ]
    attended, attn_back = jax.vjp(
        functools.partial(attention_core, segment=document_numbers), queries, keys_pre, values_pre
    )
    (heads_half,) = exchange(2, [("gather", attended.reshape(length, -1).astype(BF))], 25)
    (attn_sum,) = exchange(
        3, [("rowsum", matrix_product(heads_half, attn_out_flat).astype(BF))], 5
    )
    attn_stream = concat + attn_sum
    x_two, sum_two = exchange(
        4,
        [
            ("gather2", (attn_stream * mlp_gain).astype(BF)),
            ("colsum", pack_rows(jnp.sum(attn_stream * attn_stream, 1))),
        ],
        25,
    )
    scale_two = lax.rsqrt(sum_two.reshape(-1) / concat_width + EPS)[:, None]
    norm_two = attn_stream * scale_two
    normed_two = (x_two.astype(F32) * scale_two).astype(BF)
    adapter_middle = matrix_product(normed_two, down_full)
    gate_up_local = jnp.einsum("tk,iko->ito", normed_two, gate_up_t, preferred_element_type=F32)
    gate_up_local = gate_up_local + jnp.einsum(
        "gb,sbm->sgm", adapter_middle, adapter_up_broad, precision=FULL_PRECISION
    )
    hidden_own = gelu_product(gate_up_local[0], gate_up_local[1]).astype(BF)
    (hidden_half,) = exchange(5, [("gather", hidden_own)], 45)
    (mlp_sum,) = exchange(6, [("rowsum", matrix_product(hidden_half, down_flat).astype(BF))], 5)
    mixed_b = (attn_stream + mlp_sum).astype(BF)
    half_tokens = lax.dynamic_slice_in_dim(mixed_b, row * (length // 2), length // 2, 0)
    (proj_sum,) = exchange(7, [("scatter2", matrix_product(half_tokens, proj_flat).astype(BF))], 15)
    resid = hidden_state_input.astype(F32) + proj_sum
    x_three, sum_three = exchange(
        8,
        [
            ("gather2", (resid * mixer_norm_gain).astype(BF)),
            ("colsum", pack_rows(jnp.sum(resid * resid, 1))),
        ],
        15,
    )
    scale_three = lax.rsqrt(sum_three.reshape(-1) / model_width + EPS)[:, None]
    norm_three = resid * scale_three
    normed_three = (x_three.astype(F32) * scale_three).astype(BF)
    zx_own = jnp.einsum("tk,iko->ito", normed_three, gate_in_t, preferred_element_type=F32)
    bcdt = matrix_product(normed_three, state_in_full)
    state_cols = state_conv_kernel.shape[1]
    heads_own = step_offset_bias.shape[0]
    owner = row * n + col
    step_own = lax.dynamic_slice_in_dim(bcdt, state_cols + owner * heads_own, heads_own, 1)
    docs = jnp.cumsum(document_start_flags) - 1
    bc_conv, bc_back = jax.vjp(
        functools.partial(bc_activate, docs=docs), bcdt[:, :state_cols], state_conv_kernel
    )
    gated, core_back = jax.vjp(
        functools.partial(mixer_core, docs=docs),
        zx_own[1],
        zx_own[0],
        step_own,
        bc_conv,
        mixer_input_kernel,
        step_offset_bias,
        log_decay_rates,
        head_skip_term,
    )
    grad_hat = d_normed_four * gated_norm_gain
    (sums_four,) = exchange(
        9,
        [("allsum", pack_rows(jnp.sum(gated * gated, 1), jnp.sum(grad_hat * gated, 1)))],
        6,
    )
    square_four, cross_four = unpack_rows(sums_four, 2)
    scale_four = lax.rsqrt(square_four / inner_width + EPS)[:, None]
    norm_four = gated * scale_four
    inner_four = cross_four[:, None] * scale_four / inner_width
    d_gated = scale_four * (grad_hat - norm_four * inner_four)
    grad_gated_gain = jnp.sum(d_normed_four * norm_four, 0)
    normed_half = lax.all_gather(
        (norm_four * gated_norm_gain).astype(BF)[None], "col", axis=2, tiled=True
    )[0]
    out_sum = lax.psum(matrix_product(normed_half, mixer_out_matrix).astype(BF), "row")
    block_out = (resid + out_sum.astype(F32)).astype(BF)
    grad_mixer_out_matrix = matmul_tn(normed_half, output_gradient)

    (
        d_x_pre,
        d_gate_z,
        d_step_own,
        d_bc_part,
        grad_mixer_input_kernel,
        grad_step_offset_bias,
        grad_log_decay,
        grad_head_skip,
    ) = core_back(d_gated)
    step_slot = lax.dynamic_update_slice_in_dim(
        jnp.zeros((length, state_width - state_cols), F32), d_step_own, owner * heads_own, 1
    )
    d_bc_pre, grad_state_conv_kernel = bc_back(d_bc_part)
    d_bcdt_b = jnp.concatenate([d_bc_pre, step_slot], 1).astype(BF)
    d_zx_own = jnp.stack([d_gate_z, d_x_pre]).astype(BF)
    partial_three = jnp.einsum(
        "ito,iko->tk", d_zx_own, gate_in_t, preferred_element_type=F32
    ) + matrix_product_transposed(d_bcdt_b, state_in_full)
    cross_three = jnp.sum(d_zx_own.astype(F32) * zx_own, (0, 2)) + jnp.sum(
        d_bcdt_b.astype(F32) * bcdt, 1
    )
    d_normed_three, inner_three = exchange(
        10, [("reduce", partial_three.astype(BF)), ("allsum", pack_rows(cross_three))], 18
    )

    def returned(grad, ident, micros):
        outer, own = grad.shape[0], grad.shape[2]
        shaped = grad.astype(BF).reshape(outer, n, -1, width, own).transpose(1, 0, 2, 3, 4)
        lead = shaped.shape[1] * shaped.shape[2]
        shaped = shaped.reshape(n, lead, width, own)
        share = lax.psum_scatter(shaped, "dp", scatter_dimension=2, tiled=True)
        (back,) = exchange(ident, [("a2a_back", share.reshape(n, -1, own))], micros)
        full = lax.all_gather(
            back.reshape(lead, -1, n * own), "dp", axis=1, tiled=True
        )
        return full.astype(F32)

    def dp_sum(grad):
        return lax.psum(grad.astype(BF), "dp").astype(F32)

    def norm_back(grad_in, inner, normal, scale, gain, count):
        mean = inner.reshape(-1)[:, None] / count
        return scale * (grad_in * gain - normal * mean), jnp.sum(grad_in * normal, 0)

    grad_gate_in = jnp.einsum("tk,ito->iko", normed_three, d_zx_own, preferred_element_type=F32)
    grad_state_in_part = matmul_tn(normed_three, d_bcdt_b)
    d_norm_three, grad_mixer_gain = norm_back(
        d_normed_three, inner_three, norm_three, scale_three, mixer_norm_gain, model_width
    )
    d_resid = output_gradient.astype(F32) + d_norm_three
    (d_resid_full,) = exchange(11, [("gather2", d_resid.astype(BF))], 15)
    grad_projection_matrix = matmul_tn(mixed_b, d_resid_full)
    d_mixed = matrix_product_transposed(d_resid_full, proj_flat)
    d_mixed_b = d_mixed.astype(BF)
    grad_down_matrix = matmul_tn(hidden_half, d_mixed_b)
    (d_hidden_own,) = exchange(
        12, [("scatter", matrix_product_transposed(d_mixed_b, down_flat).astype(BF))], 45
    )
    act_back = jax.vjp(gelu_product, gate_up_local[0], gate_up_local[1])[1]
    grad_gate_up_local = jnp.stack(act_back(d_hidden_own))
    grad_adapter_up = jnp.einsum(
        "mc,ymv->ycv", adapter_middle, grad_gate_up_local, precision=FULL_PRECISION
    )
    middle_part = jnp.einsum(
        "oaj,opj->ap", grad_gate_up_local, adapter_up_broad, precision=FULL_PRECISION
    ).astype(BF)
    d_gate_up_b = grad_gate_up_local.astype(BF)
    partial_two = jnp.einsum(
        "ito,iko->tk", d_gate_up_b, gate_up_t, preferred_element_type=F32
    ) + matrix_product_transposed(middle_part, down_full)
    cross_two = jnp.sum(d_gate_up_b.astype(F32) * gate_up_local, (0, 2))
    d_normed_two, inner_two = exchange(
        13, [("reduce", partial_two.astype(BF)), ("allsum", pack_rows(cross_two))], 28
    )
    grad_gate_up = jnp.einsum("tk,ito->iko", normed_two, d_gate_up_b, preferred_element_type=F32)
    grad_adapter_down_part = matmul_tn(normed_two, middle_part)
    d_norm_two, grad_perceptron_gain = norm_back(
        d_normed_two, inner_two, norm_two, scale_two, mlp_gain, concat_width
    )
    d_attn = d_mixed + d_norm_two
    d_attn_b = d_attn.astype(BF)
    grad_attention_out = matmul_tn(heads_half, d_attn_b)
    (d_heads_own,) = exchange(
        14, [("scatter", matrix_product_transposed(d_attn_b, attn_out_flat).astype(BF))], 25
    )
    d_qkv_b = jnp.stack(
        [g.reshape(length, -1) for g in attn_back(d_heads_own.reshape(length, heads_here, head_size))]
    ).astype(BF)
    partial_one = jnp.einsum("ito,iko->tk", d_qkv_b, qkv_t, preferred_element_type=F32)
    cross_one = jnp.sum(d_qkv_b.astype(F32) * qkv_own, (0, 2))
    grad_qkv = jnp.einsum("tk,ito->iko", normed_one, d_qkv_b, preferred_element_type=F32)
    d_normed_one, inner_one = exchange(
        15, [("reduce", partial_one.astype(BF)), ("allsum", pack_rows(cross_one))], 28
    )
    d_norm_one, grad_attention_gain = norm_back(
        d_normed_one, inner_one, norm_one, scale_one, attn_gain, concat_width
    )
    d_concat = (d_attn + d_norm_one).reshape(length, 2, width)
    grad_hidden = d_resid + d_concat[:, 0]
    grad_embed = d_concat[:, 1]

    grad_gate_in_matrix = returned(grad_gate_in, 16, 15).reshape(gate_in_matrix.shape)
    grad_gate_up_matrix = returned(grad_gate_up, 17, 25).reshape(gate_up_matrix.shape)
    grad_query_key_value = returned(grad_qkv, 18, 20).reshape(query_key_value_matrix.shape)

    def own_features(summed):
        rows = summed.shape[0] // n
        return lax.dynamic_slice_in_dim(summed, col * rows, rows, 0)

    shared = lax.psum(
        (grad_state_in_part.astype(BF), grad_adapter_down_part.astype(BF)), ("dp", "row", "col")
    )
    grad_state_in_matrix = own_features(shared[0]).astype(F32)
    grad_adapter_down = own_features(shared[1]).astype(F32).reshape(adapter_down.shape)
    grad_state_conv_kernel = lax.psum(grad_state_conv_kernel, ("dp", "row", "col"))
    (
        grad_attention_gain,
        grad_perceptron_gain,
        grad_mixer_gain,
        grad_mixer_input_kernel,
        grad_step_offset_bias,
        grad_log_decay,
        grad_head_skip,
        grad_gated_gain,
    ) = lax.psum(
        (
            grad_attention_gain.reshape(attention_norm_gain.shape),
            grad_perceptron_gain.reshape(perceptron_norm_gain.shape),
            grad_mixer_gain,
            grad_mixer_input_kernel,
            grad_step_offset_bias,
            grad_log_decay,
            grad_head_skip,
            grad_gated_gain,
        ),
        "dp",
    )
    return (
        block_out,
        grad_hidden,
        grad_embed,
        grad_attention_gain,
        grad_query_key_value,
        dp_sum(grad_attention_out).reshape(attention_out_matrix.shape),
        grad_perceptron_gain,
        grad_gate_up_matrix,
        grad_adapter_down,
        dp_sum(grad_adapter_up),
        dp_sum(grad_down_matrix).reshape(down_matrix.shape),
        dp_sum(grad_projection_matrix).reshape(projection_matrix.shape),
        grad_mixer_gain,
        grad_gate_in_matrix,
        grad_state_in_matrix,
        grad_mixer_input_kernel,
        grad_state_conv_kernel,
        grad_step_offset_bias,
        grad_log_decay,
        grad_head_skip,
        grad_gated_gain,
        dp_sum(grad_mixer_out_matrix),
    )


def solution(mesh):
    tokens = P("dp", "col")
    spread = ("row", "col")
    return jax.shard_map(
        body,
        mesh=mesh,
        in_specs=(
            tokens,
            tokens,
            P("dp"),
            P("dp"),
            P(None, "col"),
            P(None, None, "col", "row"),
            P("row", None, "col"),
            P(None, "col"),
            P(None, None, "col", "row"),
            P(None, "col", None),
            P(None, None, spread),
            P("row", None, "col"),
            P(None, "col", None),
            P("col"),
            P(None, "col", "row"),
            P("col", None),
            P(None, spread),
            P(),
            P(spread),
            P(spread),
            P(spread),
            P(spread),
            P("row", "col"),
            tokens,
        ),
        out_specs=(
            tokens,
            tokens,
            tokens,
            P(None, "col"),
            P(None, None, "col", "row"),
            P("row", None, "col"),
            P(None, "col"),
            P(None, None, "col", "row"),
            P(None, "col", None),
            P(None, None, spread),
            P("row", None, "col"),
            P(None, "col", None),
            P("col"),
            P(None, "col", "row"),
            P("col", None),
            P(None, spread),
            P(),
            P(spread),
            P(spread),
            P(spread),
            P(spread),
            P("row", "col"),
        ),
        check_vma=False,
    )
```

time: 1930 us -> 1090 us (0.56)
  waiting for transfers between devices: 1430 us -> 169 us
  Pallas kernels: 0 us -> 487 us
  blocking collectives: 126 us -> 63.2 us
  matrix products: 153 us -> 128 us
    psum x10 -> x3, waiting for transfers between devices: 664 us -> 105 us  [the longest x1 105 us: dp_sum(): return lax.psum(grad.astype(BF), 'dp').astype(F32)]
    reduce_scatter x7 -> x4, waiting for transfers between devices: 503 us -> 11.6 us  [the longest x3 11.6 us: returned(): share = lax.psum_scatter(shaped, 'dp', scatter_dimension=2, tiled=True)]
    pallas_call x0 -> x19, Pallas kernels: none -> 487 us  [exchange(): pl.pallas_call(kernel, out_shape=[jax.ShapeDtypeStruct(p[1], p[2]) for p...]
    all_gather x7, waiting for transfers between devices: 260 us -> 52.1 us  [the longest x3 33.6 us: spread(): return lax.all_gather(shaped, 'dp', axis=2, tiled=True)]
    psum x9 -> x2, blocking collectives: 126 us -> 63.2 us  [the longest x1 44.6 us: body(): lax.psum(grad_state_conv_kernel, ('dp', 'row', 'col'))]
    reshape x5 -> x16, local copies, waits for them, and re-layouts: 9.02 us -> 63.6 us  [the longest x4 18 us: returned(): grad.astype(BF).reshape(outer, n, -1, width, own).transpose(1, 0, 2, 3, 4)]
    unnamed x294 -> x314, local copies, waits for them, and re-layouts: 50 us -> 12.4 us
    dot_general x17 -> x15, matrix products: 71.1 us -> 48.9 us  [the longest x6 15 us: matrix_product(): return jnp.dot(left, right, preferred_element_type=F32)]
  transfers between devices with their start and end apart: 24 -> 14, of which waited for: 22 -> 4; matrix products, arithmetic and copies ran while one was open for 9% -> 25% of each run, Pallas kernels for 0% -> 38%
where the time goes in v1:
time: 1090 us; the launch traced here: 1080 us
  Pallas kernels  487 us (45%)
  waiting for transfers between devices  169 us (16%)
  matrix products  128 us (12%)
  local copies, waits for them, and re-layouts  117 us (11%)
  other arithmetic  96.6 us (9%)
  blocking collectives  63.2 us (6%)
  between operations  18 us (2%)
    pallas_call x19, Pallas kernels, exchange(): pl.pallas_call(kernel, out_shape=[jax.ShapeDtypeStruct(p[1], p[2]) for p...  487 us
    psum x1, waiting for transfers between devices, dp_sum(): return lax.psum(grad.astype(BF), 'dp').astype(F32)  105 us
    psum x1, blocking collectives, body(): lax.psum(grad_state_conv_kernel, ('dp', 'row', 'col'))  44.6 us
    all_gather x3, waiting for transfers between devices, spread(): return lax.all_gather(shaped, 'dp', axis=2, tiled=True)  33.6 us
  transfers between devices with their start and end apart: 14, of which 4 were waited for; matrix products, arithmetic and copies ran while one was open for 25% of the time, Pallas kernels for 38%

profile of v1, /device:TPU:0, one launch (start us, length us, event | category | flops | bytes accessed | tf_op | source)
XLA Modules:
  0.0 1079.7 jit_solution(265448260884270301)
XLA Ops:
  19.2 72.3 %exchange_1.1 = (bf16[512,2048]{1,0:T(8,128)(2,1)}, f32[4,128]{1,0:T(4,128)}, bf16[4,256,512]{2,1,0:T(8,128)(2,1)}, bf16[4,128,256]{2,1,0:T(8,128)(2,1)}, bf16[5...) custom-call(bf16[512,512]{1,0:T(8,128)(2,1)} %multiply_convert_fusion.5.refs_0_, f32[4,128]{1,0:T(4,128)} %bitcast.480, ...), custom_call_target="tpu_custom_call" | custom-call | bytes 180000000 | tf_op jit(solution)/shard_map/exchange_1/pallas_call | solution.py:452
  92.5 19.7 %exchange_0.1 = bf16[4,384,256]{2,1,0:T(8,128)(2,1)} custom-call(bf16[384,1024]{1,0:T(8,128)(2,1)} %bitcast.416), custom_call_target="tpu_custom_call" | custom-call | bytes 60000000 | tf_op jit(solution)/shard_map/exchange_0/pallas_call | solution.py:452
  131.1 33.6 %all-gather.8.cloned.1.call-done = bf16[4,6,256,256]{3,2,1,0:T(8,128)(2,1)} async-done(((bf16[4,6,64,256]{3,2,1,0:T(8,128)(2,1)}), bf16[4,6,256,256]{3,2,1,0:T(8,128)(2,1)}) %all-gather.8.cloned.1.call-update) | async-done | bytes 3145744 | tf_op jit(solution)/shard_map/all_gather | solution.py:517
  190.4 23.1 %exchange_2.1 = bf16[512,1024]{1,0:T(8,128)(2,1)} custom-call(bf16[512,256]{1,0:T(8,128)(2,1)} %copy.154.refs_0_), custom_call_target="tpu_custom_call" | custom-call | bytes 75000000 | tf_op jit(solution)/shard_map/exchange_2/pallas_call | solution.py:452
  223.5 34.4 %exchange_4.1 = (bf16[512,2048]{1,0:T(8,128)(2,1)}, f32[4,128]{1,0:T(4,128)}) custom-call(bf16[512,512]{1,0:T(8,128)(2,1)} %multiply_convert_fusion.4.refs_0_, f32[4,128]{1,0:T(4,128)} %bitcast.489), custom_call_target="tpu_custom_call" | custom-call | bytes 75000000 | tf_op jit(solution)/shard_map/exchange_4/pallas_call | solution.py:452
  284.2 41.3 %exchange_5.1 = bf16[512,2048]{1,0:T(8,128)(2,1)} custom-call(bf16[512,512]{1,0:T(8,128)(2,1)} %multiply_convert_fusion.3.refs_0_), custom_call_target="tpu_custom_call" | custom-call | bytes 135000000 | tf_op jit(solution)/shard_map/exchange_5/pallas_call | solution.py:452
  337.4 26.9 %exchange_7.1 = f32[512,256]{1,0:T(8,128)} custom-call(bf16[256,1024]{1,0:T(8,128)(2,1)} %convolution_convert_fusion.10.refs_0_), custom_call_target="tpu_custom_call" | custom-call | bytes 45000000 | tf_op jit(solution)/shard_map/exchange_7/pallas_call | solution.py:452
  366.7 20.0 %exchange_8.1 = (bf16[512,1024]{1,0:T(8,128)(2,1)}, f32[4,128]{1,0:T(4,128)}) custom-call(bf16[512,256]{1,0:T(8,128)(2,1)} %get-tuple-element.170.refs_0_, f32[4,128]{1,0:T(4,128)} %bitcast.482), custom_call_target="tpu_custom_call" | custom-call | bytes 45000000 | tf_op jit(solution)/shard_map/exchange_8/pallas_call | solution.py:452
  465.5 18.4 %all-gather.14.cloned.1.call-done = bf16[1,512,1024]{1,2,0:T(8,128)(2,1)} async-done(((bf16[1,512,256]{1,2,0:T(8,128)(2,1)}), bf16[1,512,1024]{1,2,0:T(8,128)(2,1)}) %all-gather.14.cloned.1.call-update) | async-done | bytes 1048592 | tf_op jit(solution)/shard_map/all_gather | solution.py:654
  491.2 17.7 %exchange_10.1 = (f32[512,256]{1,0:T(8,128)}, f32[4,128]{1,0:T(4,128)}) custom-call(bf16[512,1024]{1,0:T(8,128)(2,1)} %fusion.11.refs_0_, f32[4,128]{1,0:T(4,128)} %add_bitcast_fusion.2.refs_1_), custom_call_target="tpu_custom_call" | custom-call | bytes 54000000 | tf_op jit(solution)/shard_map/exchange_10/pallas_call | solution.py:452
  512.7 17.9 %exchange_11.1 = bf16[512,1024]{1,0:T(8,128)(2,1)} custom-call(bf16[512,256]{1,0:T(8,128)(2,1)} %get-tuple-element.136.refs_0_), custom_call_target="tpu_custom_call" | custom-call | bytes 45000000 | tf_op jit(solution)/shard_map/exchange_11/pallas_call | solution.py:452
  535.8 42.6 %exchange_12.1 = f32[512,512]{1,0:T(8,128)} custom-call(bf16[512,2048]{1,0:T(8,128)(2,1)} %convolution_convert_fusion.2.refs_0_), custom_call_target="tpu_custom_call" | custom-call | bytes 135000000 | tf_op jit(solution)/shard_map/exchange_12/pallas_call | solution.py:452
  594.1 38.1 %exchange_13.1 = (f32[512,512]{1,0:T(8,128)}, f32[4,128]{1,0:T(4,128)}) custom-call(bf16[512,2048]{1,0:T(8,128)(2,1)} %fusion.refs_0_, f32[4,128]{1,0:T(4,128)} %bitcast.481), custom_call_target="tpu_custom_call" | custom-call | bytes 84000000 | tf_op jit(solution)/shard_map/exchange_13/pallas_call | solution.py:452
  637.2 28.9 %exchange_14.1 = f32[512,256]{1,0:T(8,128)} custom-call(bf16[512,1024]{1,0:T(8,128)(2,1)} %convolution_convert_fusion.8.refs_0_), custom_call_target="tpu_custom_call" | custom-call | bytes 75000000 | tf_op jit(solution)/shard_map/exchange_14/pallas_call | solution.py:452
  695.1 8.6 copy.126
  718.9 11.2 %copy.129 = bf16[4,2,2,256,512]{4,3,2,1,0:T(8,128)(2,1)} copy(bf16[4,2,2,256,512]{3,2,0,4,1:T(2,128)(2,1)} %bitcast.395) | data formatting | bytes 8388608 | tf_op jit(solution)/shard_map/transpose | solution.py:689
  737.0 15.5 %exchange_16.1 = bf16[128,1024]{1,0:T(8,128)(2,1)} custom-call(bf16[4,128,256]{2,1,0:T(8,128)(2,1)} %bitcast.461), custom_call_target="tpu_custom_call" | custom-call | bytes 45000000 | tf_op jit(solution)/shard_map/exchange_16/pallas_call | solution.py:452
  778.8 19.8 %exchange_18.1 = bf16[384,1024]{1,0:T(8,128)(2,1)} custom-call(bf16[4,384,256]{2,1,0:T(8,128)(2,1)} %bitcast.457), custom_call_target="tpu_custom_call" | custom-call | bytes 60000000 | tf_op jit(solution)/shard_map/exchange_18/pallas_call | solution.py:452
  798.9 11.6 %reduce-scatter.9.cloned.1.call-done = bf16[4,4,64,512]{3,2,1,0:T(8,128)(2,1)} async-done(((bf16[4,4,256,512]{3,2,1,0:T(8,128)(2,1)}), bf16[4,4,64,512]{3,2,1,0:T(8,128)(2,1)}) %reduce-scatter.9.cloned.1.call-update) | async-done | bytes 1048592 | tf_op jit(solution)/shard_map/reduce_scatter | solution.py:692
  810.4 23.3 %exchange_17.1 = bf16[256,2048]{1,0:T(8,128)(2,1)} custom-call(bf16[4,256,512]{2,1,0:T(8,128)(2,1)} %bitcast.450), custom_call_target="tpu_custom_call" | custom-call | bytes 75000000 | tf_op jit(solution)/shard_map/exchange_17/pallas_call | solution.py:452
  833.8 44.6 %psum.130 = f32[4,128]{1,0:T(4,128)} all-reduce(f32[4,128]{1,0:T(4,128)S(1)} %pad_add_fusion.1), channel_id=1, replica_groups=mesh['dp'=4,'row'=2,'col'=4] {'dp','row','col'}, use_global_device_ids=true, to_apply=%region_47.48 | all-reduce | flops 512 | bytes 4096 | tf_op jit(solution)/shard_map/psum | solution.py:776
  884.5 30.1 %exchange_15.1 = (f32[512,512]{1,0:T(8,128)}, f32[4,128]{1,0:T(4,128)}) custom-call(bf16[512,2048]{1,0:T(8,128)(2,1)} %bitcast_convert_fusion.refs_0_, f32[4,128]{1,0:T(4,128)} %bitcast.488), custom_call_target="tpu_custom_call" | custom-call | bytes 84000000 | tf_op jit(solution)/shard_map/exchange_15/pallas_call | solution.py:452
  919.7 18.6 %all-reduce.29 = (f32[2,256]{1,0:T(2,128)}, f32[2,256]{1,0:T(2,128)}, f32[256]{0:T(256)}, f32[4,256]{1,0:T(4,128)}, f32[4]{0:T(128)}, /*index=5*/f32[4]{0:T(128)}, f32[4]{0:T(128)}, f32[256]{0:T(256)}) all-reduce(f32[2,256]{1,0:T(2,128)S(1)} %reshape.742, ...), channel_id=1, replica_groups=mesh['dp'=4,'row'=2,'col'=4] {'dp'}, use_global_device_ids=true, to_apply=%region_24.25 | all-reduce | flops 2572 | bytes 20576 | tf_op jit(solution)/shard_map/psum | solution.py:786
  945.1 104.6 %all-reduce.40.cloned.1.call-done = (bf16[2,128,512]{1,2,0:T(8,128)(2,1)}, bf16[1024,2,256]{2,1,0:T(2,128)(2,1)}, bf16[2048,2,256]{2,1,0:T(2,128)(2,1)}, bf16[2,256,1024]{2,1,0:T(8,128)(2,1)}, bf16[1024,256]{1,0:T(8,128)(2,1)}) async-done(((bf16[2,128,512]{1,2,0:T(8,128)(2,1)}, bf16[1024,2,256]{2,1,0:T(2,128)(2,1)}, bf16[2048,2,256]{2,1,0:T(2,128)(2,1)}, bf16[2,256,1024]{2,1,0:T(8,128)(2,1)}, ...) | async-done | bytes 4980752 | tf_op jit(solution)/shard_map/psum | solution.py:700
  (529 shorter events, 338.8 us)
Async XLA Ops:
  8.0 83.5 %copy-start = (bf16[3,2,256,1024]{3,2,1,0:T(8,128)(2,1)S(1)}, bf16[3,2,256,1024]{3,2,1,0:T(8,128)(2,1)}, u32[]{:S(2)}) copy-start(bf16[3,2,256,1024]{3,2,1,0:T(8,128)(2,1)} %param.29) | copy-start | bytes 9437188
  8.0 119.7 %all-gather.12.cloned.1.call-start = ((), (), s32[]{:S(2)}) async-start(), calls=%async_computation.6 | async-start | bytes 1310720 | tf_op jit(solution)/shard_map/all_gather | solution.py:517
  91.5 73.3 %all-gather.8.cloned.1.call-start = ((), (), s32[]{:S(2)}) async-start(), calls=%async_computation.4 | async-start | bytes 3932160 | tf_op jit(solution)/shard_map/all_gather | solution.py:517
  112.2 148.7 %all-gather.10.cloned.1.call-start = ((), (), s32[]{:S(2)}) async-start(), calls=%async_computation.5 | async-start | bytes 5242880 | tf_op jit(solution)/shard_map/all_gather | solution.py:517
  113.0 294.9 %reduce-scatter.5.cloned.1.call-start = ((), (), s32[]{:S(2)}) async-start(), calls=%async_computation.7 | async-start | bytes 1310720 | tf_op jit(solution)/shard_map/reduce_scatter | solution.py:563
  114.6 369.3 %all-gather.14.cloned.1.call-start = ((), (), s32[]{:S(2)}) async-start(), calls=%async_computation.8 | async-start | bytes 1310720 | tf_op jit(solution)/shard_map/all_gather | solution.py:654
  116.7 277.8 %copy-start.132 = (f32[4]{0:T(128)}, f32[4]{0:T(128)S(1)}, u32[]{:S(2)}) copy-start(f32[4]{0:T(128)S(1)} %exponential_negate_fusion) | copy-start | bytes 52
  123.8 272.4 %copy-start.116 = (f32[128]{0:T(128)}, f32[128]{0:T(128)S(1)}, u32[]{:S(2)}) copy-start(f32[128]{0:T(128)S(1)} %get-tuple-element.195) | copy-start | bytes 1540
  222.5 111.4 %copy-start.6 = (f32[512,512]{1,0:T(8,128)}, f32[512,512]{1,0:T(8,128)S(1)}, u32[]{:S(2)}) copy-start(f32[512,512]{1,0:T(8,128)S(1)} %get-tuple-element.145) | copy-start | bytes 3145732
  455.9 53.9 %all-reduce.36.cloned.1.call-start = ((), (), s32[]{:S(2)}) async-start(), calls=%async_computation.9 | async-start | bytes 524288 | tf_op jit(solution)/shard_map/psum | solution.py:657
  486.5 250.5 %reduce-scatter.11.cloned.1.call-start = ((), (), s32[]{:S(2)}) async-start(), calls=%async_computation.14 | async-start | bytes 1310720 | tf_op jit(solution)/shard_map/reduce_scatter | solution.py:692
  509.6 269.2 %reduce-scatter.7.cloned.1.call-start = ((), (), s32[]{:S(2)}) async-start(), calls=%async_computation.10 | async-start | bytes 3932160 | tf_op jit(solution)/shard_map/reduce_scatter | solution.py:692
  703.8 106.6 %reduce-scatter.9.cloned.1.call-start = ((), (), s32[]{:S(2)}) async-start(), calls=%async_computation.12 | async-start | bytes 5242880 | tf_op jit(solution)/shard_map/reduce_scatter | solution.py:692
  730.1 209.0 %all-reduce.38.cloned.1.call-start = ((), (), s32[]{:S(2)}) async-start(), calls=%async_computation.16 | async-start | bytes 1703936 | tf_op jit(solution)/shard_map/psum | solution.py:771
  736.9 205.4 %all-gather.20.cloned.1.call-start = ((), (), s32[]{:S(2)}) async-start(), calls=%async_computation.15 | async-start | bytes 1310720 | tf_op jit(solution)/shard_map/all_gather | solution.py:694
  752.6 297.1 %all-reduce.40.cloned.1.call-start = ((), (), s32[]{:S(2)}) async-start(), calls=%async_computation.17 | async-start | bytes 9961472 | tf_op jit(solution)/shard_map/psum | solution.py:700
  778.7 281.0 %all-gather.16.cloned.1.call-start = ((), (), s32[]{:S(2)}) async-start(), calls=%async_computation.11 | async-start | bytes 3932160 | tf_op jit(solution)/shard_map/all_gather | solution.py:694
  798.7 79.8 %copy-start.121 = (f32[256]{0:T(256)S(1)}, f32[256]{0:T(256)}, u32[]{:S(2)}) copy-start(f32[256]{0:T(256)} %get-tuple-element.129) | copy-start | bytes 3076
  798.7 79.8 %copy-start.142 = (f32[4]{0:T(128)S(1)}, f32[4]{0:T(128)}, u32[]{:S(2)}) copy-start(f32[4]{0:T(128)} %get-tuple-element.188) | copy-start | bytes 52
  798.7 79.8 %copy-start.14 = (f32[3,512,256]{1,2,0:T(8,128)S(1)}, f32[3,512,256]{1,2,0:T(8,128)}, u32[]{:S(2)}) copy-start(f32[3,512,256]{1,2,0:T(8,128)} %copy-done.13) | copy-start | bytes 4718596
  798.8 79.8 %copy-start.43 = (bf16[512,2,128]{0,2,1:T(8,128)(2,1)S(1)}, bf16[512,2,128]{0,2,1:T(8,128)(2,1)}, u32[]{:S(2)}) copy-start(bf16[512,2,128]{0,2,1:T(8,128)(2,1)} %copy-done.42) | copy-start | bytes 786436
  798.8 79.8 %copy-start.45 = (bf16[512,2,128]{0,2,1:T(8,128)(2,1)S(1)}, bf16[512,2,128]{0,2,1:T(8,128)(2,1)}, u32[]{:S(2)}) copy-start(bf16[512,2,128]{0,2,1:T(8,128)(2,1)} %copy-done.44) | copy-start | bytes 786436
  798.8 79.8 %copy-start.91 = (bf16[2,128,512]{2,1,0:T(8,128)(2,1)S(1)}, bf16[2,128,512]{2,1,0:T(8,128)(2,1)}, u32[]{:S(2)}) copy-start(bf16[2,128,512]{2,1,0:T(8,128)(2,1)} %copy-done.90) | copy-start | bytes 786436
  798.8 266.3 %all-gather.18.cloned.1.call-start = ((), (), s32[]{:S(2)}) async-start(), calls=%async_computation.13 | async-start | bytes 5242880 | tf_op jit(solution)/shard_map/all_gather | solution.py:694
  (141 other events, 1501.9 us)
Sparse Core Ops, SparseCore 0:
  91.6 27.3 all-gather.11
  120.9 43.8 all-gather.7
  166.6 52.5 all-gather.9
  509.8 29.6 reduce-scatter.10
  703.9 49.8 reduce-scatter.6
  757.2 53.2 reduce-scatter.8
  812.3 26.6 all-gather.19
  840.8 45.1 all-gather.15
  887.9 53.4 all-gather.17
Sparse Core Ops, SparseCore 1:
  115.8 31.3 reduce-scatter.4
  455.9 27.9 all-gather.13
  486.7 17.2 all-reduce.35
  737.0 179.2 all-reduce.37
  921.7 128.0 all-reduce.39
